TPU v7x, 256 devices: a whole 4x4x8 slice. The times are simulated.
256 devices in a mesh: row: 8 (over x, core), col: 32 (over y, z).
Axes of the slice: x: 4, y: 4, z: 8, core: 2. Of those that a mesh axis runs over, the one named last changes fastest.
Arguments:
- embeddings: bfloat16 [32768, 512], P(('row', 'col')), may hold values from -6 to 6
- sketch: bfloat16 [32768, 64], P(('row', 'col')), may hold values from -240 to 240
Outputs:
- basis: float32 [32768, 64], P(('row', 'col'))
- first_pass: float32 [32768, 64], P(('row', 'col'))
All inputs are finite; a program needn't handle non-finite values.
Results may differ from a plain program's by a relative error of at most 0.00205.
Values may be sent and summed in bfloat16 or wider, within the bound.
A program may use at most 64 MiB of HBM per device.

v0:
```python
import jax
import jax.numpy as jnp
from jax import lax
from jax.sharding import Mesh
from jax.sharding import PartitionSpec as P

ROW = ("row_0", "row_1")
COL = ("col_0", "col_1")
ROW_COL = ("row_0", "row_1", "col_0", "col_1")


def in_order(blocks, dim):
    blocks = jnp.moveaxis(blocks, 0, dim)
    dims = blocks.shape
    return blocks.reshape(*dims[:dim], dims[dim] * dims[dim + 1], *dims[dim + 2 :])


def from_everyone(shard, axis):
    copies = jnp.broadcast_to(shard, (lax.axis_size(axis), *shard.shape))
    return lax.all_to_all(copies, axis, split_axis=0, concat_axis=0, tiled=True)


def gather_directly(shard, axis, dim):
    return in_order(from_everyone(shard, axis), dim)


def in_blocks(shard, dim, length):
    dims = shard.shape
    blocks = shard.reshape(*dims[:dim], length, dims[dim] // length, *dims[dim + 1 :])
    return jnp.moveaxis(blocks, dim, 0)


def sent_and_summed(shard, axis, dim):
    length = lax.axis_size(axis)
    blocks = lax.all_to_all(in_blocks(shard, dim, length), axis, 0, 0, tiled=True)
    return jnp.sum(blocks, axis=0)


def over_copies(shard, axis):
    return from_everyone(shard, axis).sum(axis=0)


def one_axis_at_a_time(shard, axes):
    far, near = axes
    return over_copies(over_copies(shard, near), far)


def squares_of(points):
    return jnp.sum(jnp.square(points.astype(jnp.float32)), axis=1)


def kernel_tile(left, right, left_sq, right_sq, gamma):
    cross = lax.dot_general(
        left, right, (((1,), (1,)), ((), ())), preferred_element_type=jnp.float32
    )
    dist = left_sq[:, None] + right_sq[None, :] - 2.0 * cross
    return jnp.exp(-gamma * dist).astype(jnp.bfloat16)


def product_of(left, right):
    return lax.dot_general(
        left,
        right,
        (((0,), (0,)), ((), ())),
        precision=lax.Precision.HIGHEST,
        preferred_element_type=jnp.float32,
    )


def per_device(embeddings, sketch):
    width = embeddings.shape[1]
    gamma = 3.0 / width
    own_points = gather_directly(embeddings, ROW, 0)
    own_sq = squares_of(own_points)
    empty = jnp.zeros((own_points.shape[0], sketch.shape[1]), jnp.float32)
    total = empty
    points = lax.all_gather(embeddings, COL, axis=0, tiled=True)
    tests = lax.all_gather(sketch, COL, axis=0, tiled=True)
    count = points.shape[0]
    size = 512

    def step(carry, block):
        block_points, block_tests = block
        tile = kernel_tile(own_points, block_points, own_sq, squares_of(block_points), gamma)
        return (carry + jnp.dot(tile, block_tests, preferred_element_type=jnp.float32), None)

    stacked = (
        points.reshape(count // size, size, width),
        tests.reshape(count // size, size, tests.shape[1]),
    )
    total, unused = lax.scan(step, total, stacked)
    sketched = sent_and_summed(total, ROW, 0)
    core = one_axis_at_a_time(
        product_of(sketch.astype(jnp.float32), sketched), (("row_0", "row_1"), ("col_0", "col_1"))
    )
    lower = jnp.linalg.cholesky(core)
    first = jax.scipy.linalg.solve_triangular(lower, sketched.T, lower=True).T
    gram_two = one_axis_at_a_time(
        product_of(first, first), (("row_0", "row_1"), ("col_0", "col_1"))
    )
    lower_two = jnp.linalg.cholesky(gram_two)
    second = jax.scipy.linalg.solve_triangular(lower_two, first.T, lower=True).T
    total_points = sketched.shape[0] * lax.axis_size(ROW) * lax.axis_size(COL)
    scale = jnp.sqrt(jnp.float32(total_points))
    return (second * scale, first * scale)


def solution(mesh):
    torus = Mesh(mesh.devices.reshape(4, 2, 4, 8), ("row_0", "row_1", "col_0", "col_1"))
    in_specs = (P(ROW_COL, None), P(ROW_COL, None))
    out_specs = (P(ROW_COL, None), P(ROW_COL, None))
    return jax.shard_map(
        per_device, mesh=torus, in_specs=in_specs, out_specs=out_specs, check_vma=False
    )
```

profile of v0, /device:TPU:32, one launch (start us, length us, event | category | flops | bytes accessed | tf_op | source)
XLA Modules:
  0.0 239.0 jit_solution(14531047242678938613)
XLA Ops:
  7.9 2.0 broadcast_in_dim.22
  9.9 4.3 %all-to-all-start = ((bf16[8,128,512]{2,1,0:T(8,128)(2,1)}), bf16[8,128,512]{2,1,0:T(8,128)(2,1)S(1)}, u32[]{:S(2)}, u32[]{:S(2)}) async-start(bf16[8,128,512]{2,1,0:T(8,128)(2,1)} %broadcast_in_dim.22), calls=%async_computation | async-start | bytes 2097152 | tf_op jit(solution)/shard_map/all_to_all | solution.py:20
  14.2 52.8 %all_gather.7 = bf16[4096,64]{0,1:T(8,128)(2,1)S(1)} all-gather(bf16[128,64]{0,1:T(8,128)(2,1)S(1)} %copy-done), channel_id=1, replica_groups=mesh['row_0'=4,'row_1'=2,'col_0'=4,'col_1'=8] {'col_0','col_1'}, dimensions={0}, use_global_device_ids=true | all-gather | bytes 540672 | tf_op jit(solution)/shard_map/all_gather | solution.py:78
  67.8 27.1 %all-gather.2.cloned.1.call-done = bf16[4096,512]{1,0:T(8,128)(2,1)} async-done(((bf16[128,512]{1,0:T(8,128)(2,1)}), bf16[4096,512]{1,0:T(8,128)(2,1)}) %all-gather.2.cloned.1.call-update) | async-done | bytes 4194320 | tf_op jit(solution)/shard_map/all_gather | solution.py:77
  94.9 26.7 %while.11 = (s32[]{:T(128)}, f32[1024,64]{0,1:T(8,128)S(1)}, f32[1024]{0:T(1024)S(1)}, bf16[8,512,512]{2,1,0:T(8,128)(2,1)}, bf16[1024,512]{1,0:T(8,128)(2,1)S(1...) while((s32[]{:T(128)}, f32[1024,64]{0,1:T(8,128)S(1)}, f32[1024]{0:T(1024)S(1)}, ...), condition=%wide.region_3.4_spmd.clone, body=%wide.region_1.3_spmd.clone.sunk | while | flops 607518208 | bytes 2761827 | solution.py:91
  96.1 2.1 fusion.45
  99.4 2.1 fusion.45
  102.8 2.1 fusion.45
  106.1 2.1 fusion.45
  109.4 2.1 fusion.45
  112.8 2.1 fusion.45
  116.1 2.1 fusion.45
  119.4 2.1 fusion.45
  121.6 11.6 %all_to_all.30 = f32[8,128,64]{1,2,0:T(8,128)S(1)} all-to-all(f32[8,128,64]{1,2,0:T(8,128)S(1)} %copy_bitcast_fusion), channel_id=1, replica_groups=mesh['row_0'=4,'row_1'=2,'col_0'=4,'col_1'=8] {'row_0','row_1'}, dimensions={0} | all-to-all | bytes 524288 | tf_op jit(solution)/shard_map/all_to_all | solution.py:35
  134.2 22.9 %all_to_all.31 = f32[32,1,4096]{2,1,0:T(1,128)S(1)} all-to-all(f32[32,1,4096]{2,1,0:T(1,128)S(1)} %reshape.31), channel_id=1, replica_groups=mesh['row_0'=4,'row_1'=2,'col_0'=4,'col_1'=8] {'col_0','col_1'}, dimensions={0} | all-to-all | bytes 1048576 | tf_op jit(solution)/shard_map/all_to_all | solution.py:20
  160.3 8.5 %all_to_all.32 = f32[8,1,4096]{2,1,0:T(1,128)S(1)} all-to-all(f32[8,1,4096]{2,1,0:T(1,128)S(1)} %reshape.33), channel_id=1, replica_groups=mesh['row_0'=4,'row_1'=2,'col_0'=4,'col_1'=8] {'row_0','row_1'}, dimensions={0} | all-to-all | bytes 262144 | tf_op jit(solution)/shard_map/all_to_all | solution.py:20
  169.9 5.8 %cholesky.44 = f32[64,64]{1,0:T(8,128)S(1)} custom-call(f32[64,64]{1,0:T(8,128)S(1)} %fusion.27), custom_call_target="Cholesky" | custom-call | tf_op jit(solution)/shard_map/jit(cholesky)/cholesky | solution.py:96
  177.1 4.9 %custom-call.7 = f32[1,64,64]{1,2,0:T(8,128)S(1)} custom-call(f32[1,64,64]{2,1,0:T(8,128)S(1)} %fusion.20), custom_call_target="InvertDiagBlocksLowerTriangular" | custom-call | tf_op jit(solution)/shard_map/jit(_solve_triangular)/triangular_solve | solution.py:97
  183.3 22.1 %all_to_all.33 = f32[32,1,4096]{2,1,0:T(1,128)S(1)} all-to-all(f32[32,1,4096]{2,1,0:T(1,128)S(1)} %reshape.35), channel_id=1, replica_groups=mesh['row_0'=4,'row_1'=2,'col_0'=4,'col_1'=8] {'col_0','col_1'}, dimensions={0} | all-to-all | bytes 1048576 | tf_op jit(solution)/shard_map/all_to_all | solution.py:20
  205.3 1.9 reduce.7
  208.6 3.5 %all-to-all-start.5 = ((f32[8,1,4096]{2,1,0:T(1,128)}), f32[8,1,4096]{2,1,0:T(1,128)S(1)}, u32[]{:S(2)}, u32[]{:S(2)}) async-start(f32[8,1,4096]{2,1,0:T(1,128)} %reshape.37), calls=%async_computation.5 | async-start | bytes 262144 | tf_op jit(solution)/shard_map/all_to_all | solution.py:20
  212.8 5.2 %all-to-all-done.5 = f32[8,1,4096]{2,1,0:T(1,128)S(1)} async-done(((f32[8,1,4096]{2,1,0:T(1,128)}), f32[8,1,4096]{2,1,0:T(1,128)S(1)}, u32[]{:S(2)}, u32[]{:S(2)}) %all-to-all-start.5) | async-done | bytes 131104 | tf_op jit(solution)/shard_map/all_to_all | solution.py:20
  219.2 5.8 %cholesky.55 = f32[64,64]{1,0:T(8,128)S(1)} custom-call(f32[64,64]{1,0:T(8,128)S(1)} %fusion.23), custom_call_target="Cholesky" | custom-call | tf_op jit(solution)/shard_map/jit(cholesky)/cholesky | solution.py:101
  226.4 4.9 %custom-call.8 = f32[1,64,64]{1,2,0:T(8,128)S(1)} custom-call(f32[1,64,64]{2,1,0:T(8,128)S(1)} %fusion.21), custom_call_target="InvertDiagBlocksLowerTriangular" | custom-call | tf_op jit(solution)/shard_map/jit(_solve_triangular)/triangular_solve | solution.py:102
  (54 shorter events, 24.4 us)
Async XLA Ops:
  7.2 7.0 %copy-start = (bf16[128,64]{0,1:T(8,128)(2,1)S(1)}, bf16[128,64]{0,1:T(8,128)(2,1)}, u32[]{:S(2)}) copy-start(bf16[128,64]{0,1:T(8,128)(2,1)} %param.8) | copy-start | bytes 49156
  7.2 87.7 %all-gather.2.cloned.1.call-start = ((), (), s32[]{:S(2)}) async-start(), calls=%async_computation.6 | async-start | bytes 4325376 | tf_op jit(solution)/shard_map/all_gather | solution.py:77
  9.9 57.6 %all-to-all-start = ((bf16[8,128,512]{2,1,0:T(8,128)(2,1)}), bf16[8,128,512]{2,1,0:T(8,128)(2,1)S(1)}, u32[]{:S(2)}, u32[]{:S(2)}) async-start(bf16[8,128,512]{2,1,0:T(8,128)(2,1)} %broadcast_in_dim.22), calls=%async_computation | async-start | bytes 2097152 | tf_op jit(solution)/shard_map/all_to_all | solution.py:20
  208.6 9.4 %all-to-all-start.5 = ((f32[8,1,4096]{2,1,0:T(1,128)}), f32[8,1,4096]{2,1,0:T(1,128)S(1)}, u32[]{:S(2)}, u32[]{:S(2)}) async-start(f32[8,1,4096]{2,1,0:T(1,128)} %reshape.37), calls=%async_computation.5 | async-start | bytes 262144 | tf_op jit(solution)/shard_map/all_to_all | solution.py:20
Sparse Core Ops, SparseCore 0:
  10.6 84.2 all-gather.1
where the time goes:
time: 240 us; the launch traced here: 239 us
  blocking collectives  118 us (49%)
  other arithmetic  40.8 us (17%)
  waiting for transfers between devices  33 us (14%)
  matrix products  18.2 us (8%)
  between operations  14.3 us (6%)
  starting transfers between devices  7.89 us (3%)
  local copies, waits for them, and re-layouts  6.8 us (3%)
    all_to_all x3, blocking collectives, from_everyone(): return lax.all_to_all(copies, axis, split_axis=0, concat_axis=0, tiled=True)  53.5 us
    all_gather x1, blocking collectives, per_device(): tests = lax.all_gather(sketch, COL, axis=0, tiled=True)  52.8 us
    all_gather x1, waiting for transfers between devices, per_device(): points = lax.all_gather(embeddings, COL, axis=0, tiled=True)  27.1 us
    dot_general x8, matrix products, step(): jnp.dot(tile, block_tests, preferred_element_type=jnp.float32)  16.7 us
    all_to_all x1, blocking collectives, sent_and_summed(): lax.all_to_all(in_blocks(shard, dim, length), axis, 0, 0, tiled=True)  11.6 us
    reduce_sum x9, other arithmetic, squares_of(): return jnp.sum(jnp.square(points.astype(jnp.float32)), axis=1)  10 us
    all_to_all x2, starting transfers between devices, from_everyone(): return lax.all_to_all(copies, axis, split_axis=0, concat_axis=0, tiled=True)  7.85 us
    another operation x3, other arithmetic, per_device(): lower_two = jnp.linalg.cholesky(gram_two)  6.52 us
  transfers between devices with their start and end apart: 3, of which 2 were waited for; matrix products, arithmetic and copies ran while one was open for 1% of the time, Pallas kernels for 0%

commit v1 on v0

--- a/solution.py
+++ b/solution.py
@@ -74,8 +74,11 @@
     own_sq = squares_of(own_points)
     empty = jnp.zeros((own_points.shape[0], sketch.shape[1]), jnp.float32)
     total = empty
-    points = lax.all_gather(embeddings, COL, axis=0, tiled=True)
-    tests = lax.all_gather(sketch, COL, axis=0, tiled=True)
+    points, tests = jnp.split(
+        lax.all_gather(jnp.concatenate([embeddings, sketch], axis=1), COL, axis=0, tiled=True),
+        [embeddings.shape[1]],
+        axis=1,
+    )
     count = points.shape[0]
     size = 512
 

time: 240 us -> 249 us (1.038)
  waiting for transfers between devices: 33 us -> 86.8 us
  blocking collectives: 118 us -> 65.2 us
  local copies, waits for them, and re-layouts: 6.8 us -> 12.9 us
    all_gather x1 -> x0, blocking collectives: 52.8 us -> none  [per_device(): tests = lax.all_gather(sketch, COL, axis=0, tiled=True)]
    all_gather x1, waiting for transfers between devices: 27.1 us -> 65.7 us  [per_device(): lax.all_gather(jnp.concatenate([embeddings, sketch], axis=1), COL, axis=0...]
    all_to_all x2, waiting for transfers between devices: 5.23 us -> 21.2 us  [from_everyone(): return lax.all_to_all(copies, axis, split_axis=0, concat_axis=0, tiled=True)]
    split x0 -> x3, local copies, waits for them, and re-layouts: none -> 5.69 us  [per_device(): jnp.split(lax.all_gather(jnp.concatenate([embeddings, sketch], axis=1), C...]
  transfers between devices with their start and end apart: 3 -> 3, of which waited for: 2 -> 3; matrix products, arithmetic and copies ran while one was open for 1% -> 1% of each run, Pallas kernels for 0% -> 0%
where the time goes in v1:
time: 249 us; the launch traced here: 248 us
  waiting for transfers between devices  86.8 us (35%)
  blocking collectives  65.2 us (26%)
  other arithmetic  42.4 us (17%)
  matrix products  18.2 us (7%)
  between operations  14.3 us (6%)
  local copies, waits for them, and re-layouts  12.9 us (5%)
  starting transfers between devices  7.89 us (3%)
    all_gather x1, waiting for transfers between devices, per_device(): lax.all_gather(jnp.concatenate([embeddings, sketch], axis=1), COL, axis=0...  65.7 us
    all_to_all x3, blocking collectives, from_everyone(): return lax.all_to_all(copies, axis, split_axis=0, concat_axis=0, tiled=True)  53.6 us
    all_to_all x2, waiting for transfers between devices, from_everyone(): return lax.all_to_all(copies, axis, split_axis=0, concat_axis=0, tiled=True)  21.2 us
    dot_general x8, matrix products, step(): jnp.dot(tile, block_tests, preferred_element_type=jnp.float32)  16.7 us
    all_to_all x1, blocking collectives, sent_and_summed(): lax.all_to_all(in_blocks(shard, dim, length), axis, 0, 0, tiled=True)  11.6 us
    reduce_sum x9, other arithmetic, squares_of(): return jnp.sum(jnp.square(points.astype(jnp.float32)), axis=1)  10 us
    all_to_all x2, starting transfers between devices, from_everyone(): return lax.all_to_all(copies, axis, split_axis=0, concat_axis=0, tiled=True)  7.85 us
    another operation x3, other arithmetic, per_device(): lower = jnp.linalg.cholesky(core)  6.52 us
  transfers between devices with their start and end apart: 3, of which 3 were waited for; matrix products, arithmetic and copies ran while one was open for 1% of the time, Pallas kernels for 0%

profile of v1, /device:TPU:32, one launch (start us, length us, event | category | flops | bytes accessed | tf_op | source)
XLA Modules:
  0.0 247.8 jit_solution(10696623701706578515)
XLA Ops:
  9.7 2.0 broadcast_in_dim.22
  11.7 4.3 %all-to-all-start = ((bf16[8,128,512]{2,1,0:T(8,128)(2,1)}), bf16[8,128,512]{2,1,0:T(8,128)(2,1)S(1)}, u32[]{:S(2)}, u32[]{:S(2)}) async-start(bf16[8,128,512]{2,1,0:T(8,128)(2,1)} %broadcast_in_dim.22), calls=%async_computation | async-start | bytes 2097152 | tf_op jit(solution)/shard_map/all_to_all | solution.py:20
  16.0 15.9 %all-to-all-done = bf16[8,128,512]{2,1,0:T(8,128)(2,1)S(1)} async-done(((bf16[8,128,512]{2,1,0:T(8,128)(2,1)}), bf16[8,128,512]{2,1,0:T(8,128)(2,1)S(1)}, u32[]{:S(2)}, u32[]{:S(2)}) %all-to-all-start) | async-done | bytes 1048608 | tf_op jit(solution)/shard_map/all_to_all | solution.py:20
  32.2 65.7 %all-gather.2.cloned.1.call-done = bf16[4096,576]{1,0:T(8,128)(2,1)} async-done(((bf16[128,576]{1,0:T(8,128)(2,1)}), bf16[4096,576]{1,0:T(8,128)(2,1)}) %all-gather.2.cloned.1.call-update) | async-done | bytes 4718608 | tf_op jit(solution)/shard_map/all_gather | solution.py:78
  97.8 4.5 %split.8 = bf16[4096,512]{1,0:T(8,128)(2,1)} slice(bf16[4096,576]{1,0:T(8,128)(2,1)} %all-gather.2.cloned.1.call-done), slice={[0:4096], [0:512]} | slice | bytes 8388608 | tf_op jit(solution)/shard_map/split | solution.py:77
  103.5 26.7 %while.11 = (s32[]{:T(128)}, f32[1024,64]{0,1:T(8,128)S(1)}, f32[1024]{0:T(1024)S(1)}, bf16[8,512,512]{2,1,0:T(8,128)(2,1)}, bf16[1024,512]{1,0:T(8,128)(2,1)S(1...) while((s32[]{:T(128)}, f32[1024,64]{0,1:T(8,128)S(1)}, f32[1024]{0:T(1024)S(1)}, ...), condition=%wide.region_3.4_spmd.clone, body=%wide.region_1.3_spmd.clone.sunk | while | flops 607518208 | bytes 2761827 | solution.py:94
  104.8 2.1 fusion.45
  108.1 2.1 fusion.45
  111.4 2.1 fusion.45
  114.8 2.1 fusion.45
  118.1 2.1 fusion.45
  121.4 2.1 fusion.45
  124.8 2.1 fusion.45
  128.1 2.1 fusion.45
  130.2 11.6 %all_to_all.30 = f32[8,128,64]{1,2,0:T(8,128)S(1)} all-to-all(f32[8,128,64]{1,2,0:T(8,128)S(1)} %copy_bitcast_fusion), channel_id=1, replica_groups=mesh['row_0'=4,'row_1'=2,'col_0'=4,'col_1'=8] {'row_0','row_1'}, dimensions={0} | all-to-all | bytes 524288 | tf_op jit(solution)/shard_map/all_to_all | solution.py:35
  142.9 23.0 %all_to_all.31 = f32[32,1,4096]{2,1,0:T(1,128)S(1)} all-to-all(f32[32,1,4096]{2,1,0:T(1,128)S(1)} %reshape.31), channel_id=1, replica_groups=mesh['row_0'=4,'row_1'=2,'col_0'=4,'col_1'=8] {'col_0','col_1'}, dimensions={0} | all-to-all | bytes 1048576 | tf_op jit(solution)/shard_map/all_to_all | solution.py:20
  169.0 8.5 %all_to_all.32 = f32[8,1,4096]{2,1,0:T(1,128)S(1)} all-to-all(f32[8,1,4096]{2,1,0:T(1,128)S(1)} %reshape.33), channel_id=1, replica_groups=mesh['row_0'=4,'row_1'=2,'col_0'=4,'col_1'=8] {'row_0','row_1'}, dimensions={0} | all-to-all | bytes 262144 | tf_op jit(solution)/shard_map/all_to_all | solution.py:20
  178.7 5.8 %cholesky.44 = f32[64,64]{1,0:T(8,128)S(1)} custom-call(f32[64,64]{1,0:T(8,128)S(1)} %fusion.27), custom_call_target="Cholesky" | custom-call | tf_op jit(solution)/shard_map/jit(cholesky)/cholesky | solution.py:99
  185.9 4.9 %custom-call.7 = f32[1,64,64]{1,2,0:T(8,128)S(1)} custom-call(f32[1,64,64]{2,1,0:T(8,128)S(1)} %fusion.20), custom_call_target="InvertDiagBlocksLowerTriangular" | custom-call | tf_op jit(solution)/shard_map/jit(_solve_triangular)/triangular_solve | solution.py:100
  192.0 22.1 %all_to_all.33 = f32[32,1,4096]{2,1,0:T(1,128)S(1)} all-to-all(f32[32,1,4096]{2,1,0:T(1,128)S(1)} %reshape.35), channel_id=1, replica_groups=mesh['row_0'=4,'row_1'=2,'col_0'=4,'col_1'=8] {'col_0','col_1'}, dimensions={0} | all-to-all | bytes 1048576 | tf_op jit(solution)/shard_map/all_to_all | solution.py:20
  217.4 3.5 %all-to-all-start.5 = ((f32[8,1,4096]{2,1,0:T(1,128)}), f32[8,1,4096]{2,1,0:T(1,128)S(1)}, u32[]{:S(2)}, u32[]{:S(2)}) async-start(f32[8,1,4096]{2,1,0:T(1,128)} %reshape.37), calls=%async_computation.5 | async-start | bytes 262144 | tf_op jit(solution)/shard_map/all_to_all | solution.py:20
  221.6 5.2 %all-to-all-done.5 = f32[8,1,4096]{2,1,0:T(1,128)S(1)} async-done(((f32[8,1,4096]{2,1,0:T(1,128)}), f32[8,1,4096]{2,1,0:T(1,128)S(1)}, u32[]{:S(2)}, u32[]{:S(2)}) %all-to-all-start.5) | async-done | bytes 131104 | tf_op jit(solution)/shard_map/all_to_all | solution.py:20
  228.0 5.8 %cholesky.55 = f32[64,64]{1,0:T(8,128)S(1)} custom-call(f32[64,64]{1,0:T(8,128)S(1)} %fusion.23), custom_call_target="Cholesky" | custom-call | tf_op jit(solution)/shard_map/jit(cholesky)/cholesky | solution.py:104
  235.2 4.9 %custom-call.8 = f32[1,64,64]{1,2,0:T(8,128)S(1)} custom-call(f32[1,64,64]{2,1,0:T(8,128)S(1)} %fusion.21), custom_call_target="InvertDiagBlocksLowerTriangular" | custom-call | tf_op jit(solution)/shard_map/jit(_solve_triangular)/triangular_solve | solution.py:105
  (57 shorter events, 28.8 us)
Async XLA Ops:
  7.2 90.7 %all-gather.2.cloned.1.call-start = ((), (), s32[]{:S(2)}) async-start(), calls=%async_computation.6 | async-start | bytes 5406720 | tf_op jit(solution)/shard_map/all_gather | solution.py:78
  11.7 20.2 %all-to-all-start = ((bf16[8,128,512]{2,1,0:T(8,128)(2,1)}), bf16[8,128,512]{2,1,0:T(8,128)(2,1)S(1)}, u32[]{:S(2)}, u32[]{:S(2)}) async-start(bf16[8,128,512]{2,1,0:T(8,128)(2,1)} %broadcast_in_dim.22), calls=%async_computation | async-start | bytes 2097152 | tf_op jit(solution)/shard_map/all_to_all | solution.py:20
  102.3 1.2 slice-start
  103.5 38.3 %copy-start = (bf16[128,64]{0,1:T(8,128)(2,1)S(1)}, bf16[128,64]{0,1:T(8,128)(2,1)}, u32[]{:S(2)}) copy-start(bf16[128,64]{0,1:T(8,128)(2,1)} %param.8) | copy-start | bytes 49156
  217.4 9.4 %all-to-all-start.5 = ((f32[8,1,4096]{2,1,0:T(1,128)}), f32[8,1,4096]{2,1,0:T(1,128)S(1)}, u32[]{:S(2)}, u32[]{:S(2)}) async-start(f32[8,1,4096]{2,1,0:T(1,128)} %reshape.37), calls=%async_computation.5 | async-start | bytes 262144 | tf_op jit(solution)/shard_map/all_to_all | solution.py:20
Sparse Core Ops, SparseCore 0:
  10.5 87.2 all-gather.1
